TPU v7x, 32 devices: a whole 2x2x4 slice. The times are simulated.
32 devices in a mesh: seq: 8 (over z, x), head: 4 (over y, core).
Axes of the slice: x: 2, y: 2, z: 4, core: 2. Of those that a mesh axis runs over, the one named last changes fastest.
Arguments:
- queries: bfloat16 [8192, 2048], P('seq', 'head'), may hold values from -200 to 200
- keys: bfloat16 [8192, 2048], P('seq', 'head'), may hold values from -6 to 6
- values: bfloat16 [8192, 2048], P('seq', 'head'), may hold values from -12 to 12
- gate_bias: float32 [16], P('head'), may hold values from -2 to 2
- out_weight: bfloat16 [2048, 4096], P(None, 'head'), may hold values from -0.125 to 0.125
Outputs:
- layer_out: bfloat16 [8192, 4096], P('seq', 'head')
All inputs are finite; a program needn't handle non-finite values.
Results may differ from a plain program's by a relative error of at most 0.007.
Values may be sent and summed in bfloat16 or wider, within the bound.
A program may use at most 128 MiB of HBM per device.

v0:
```python
import jax
import jax.numpy as jnp
from jax import lax
from jax.sharding import PartitionSpec as P

DH = 128
SEG = 256


def body(queries, keys, values, gate_bias, out_weight):
    local_heads = gate_bias.shape[0]
    row_count = queries.shape[0]
    seg_count = row_count // SEG
    blk_shape = (seg_count, SEG, local_heads, DH)
    query_blk = queries.reshape(blk_shape)
    key_blk = keys.reshape(blk_shape)
    value_blk = values.reshape(blk_shape)
    high = lax.Precision.HIGHEST
    query_map = jax.nn.elu(query_blk.astype(jnp.float32)) + 1.0
    key_map = (jax.nn.elu(key_blk.astype(jnp.float32)) + 1.0).astype(jnp.bfloat16)
    deltas = jnp.einsum("sthd,sthe->shde", key_map, value_blk, preferred_element_type=jnp.float32)
    norm_sums = jnp.sum(key_map.astype(jnp.float32), axis=1)
    mem_total = jnp.sum(deltas, axis=0)
    norm_total = jnp.sum(norm_sums, axis=0)
    my_index = lax.axis_index("seq")
    pieces = (
        lax.all_gather(mem_total[None], "seq", axis=0, tiled=True),
        lax.all_gather(norm_total[None], "seq", axis=0, tiled=True),
    )
    indices = jnp.arange(pieces[0].shape[0])
    keep_mask = (indices < my_index).astype(jnp.float32)
    mem_part = jnp.sum(pieces[0] * keep_mask[:, None, None, None], axis=0)
    norm_part = jnp.sum(pieces[1] * keep_mask[:, None, None], axis=0)
    mem_inner = jnp.concatenate(
        [jnp.zeros_like(deltas[:1]), jnp.cumsum(deltas, axis=0)[:-1]], axis=0
    )
    norm_inner = jnp.concatenate(
        [jnp.zeros_like(norm_sums[:1]), jnp.cumsum(norm_sums, axis=0)[:-1]], axis=0
    )
    mem_prev = mem_part[None] + mem_inner
    norm_prev = norm_part[None] + norm_inner
    recall = jnp.einsum("sthd,shde->sthe", query_map, mem_prev, precision=high)
    denominator = jnp.einsum("sthd,shd->sth", query_map, norm_prev, precision=high) + 1.0
    recall = recall / denominator[..., None]
    positions = jnp.arange(SEG)
    causal = positions[:, None] >= positions[None, :]
    scores = jnp.einsum("sqhd,skhd->shqk", query_blk, key_blk, preferred_element_type=jnp.float32)
    scores = scores * (1.0 / DH**0.5)
    scores = jnp.where(causal[None, None], scores, jnp.float32(-1e30))
    weights = jax.nn.softmax(scores, axis=-1).astype(jnp.bfloat16)
    local_out = jnp.einsum(
        "shqk,skhd->sqhd", weights, value_blk, preferred_element_type=jnp.float32
    )
    gate_open = jax.nn.sigmoid(gate_bias)
    mixed = (
        gate_open[None, None, :, None] * recall + (1.0 - gate_open)[None, None, :, None] * local_out
    )
    context = mixed.astype(jnp.bfloat16).reshape(row_count, local_heads * DH)
    projected = jnp.dot(
        lax.all_gather(context, "head", axis=1, tiled=True),
        out_weight,
        preferred_element_type=jnp.float32,
    )
    return projected.astype(jnp.bfloat16)


def solution(mesh):
    return jax.shard_map(
        body,
        mesh=mesh,
        in_specs=(P("seq", "head"), P("seq", "head"), P("seq", "head"), P("head"), P(None, "head")),
        out_specs=P("seq", "head"),
        check_vma=False,
    )
```

profile of v0, /device:TPU:25, one launch (start us, length us, event | category | flops | bytes accessed | tf_op | source)
XLA Modules:
  0.0 121.9 jit_solution(16294287501186543389)
XLA Ops:
  6.5 0.0 copy-start.2
  6.5 0.0 all-gather.6.cloned.1.call-start
  6.5 1.4 %reshape.43 = bf16[4,256,4,128]{3,2,1,0:T(4,128)(2,1)S(1)} reshape(bf16[1024,512]{1,0:T(8,128)(2,1)} %param.6) | data formatting | bytes 2097152 | tf_op jit(solution)/shard_map/reshape | solution.py:16
  8.0 0.1 copy-done.2
  8.1 1.1 reshape.44
  9.2 0.0 copy-start.3
  9.2 4.3 %fusion.48 = (f32[4,128,128]{2,1,0:T(8,128)}, f32[4,4,128,128]{3,2,1,0:T(8,128)}) fusion(bf16[4,256,4,128]{3,2,1,0:T(4,128)(2,1)} %reshape.44, bf16[4,256,4,128]{3,2,1,0:T(4,128)(2,1)S(1)} %reshape.43), kind=kOutput, calls=%fused_computation.66 | convolution fusion | flops 137560064 | bytes 3407872 | tf_op jit(solution)/shard_map/sthd,sthe->shde/dot_general | solution.py:21
  13.5 0.0 all-gather.6.cloned.1.call-update
  13.5 0.0 all-gather.4.cloned.1.call-start
  13.5 0.0 copy-done.3
  13.5 0.3 reshape.45
  13.8 1.0 convert_reduce_fusion
  14.8 0.0 copy-start
  14.9 0.0 copy-start.5
  14.9 1.4 %fusion.49 = f32[4,4,128,128]{3,2,1,0:T(8,128)S(1)} fusion(f32[4,4,128,128]{3,2,1,0:T(8,128)} %get-tuple-element.10), kind=kOutput, calls=%fused_computation.67 | output fusion | flops 786432 | bytes 2097152 | tf_op jit(solution)/shard_map/jit(cumsum)/reduce_window_sum | solution.py:35
  16.3 0.0 copy-start.1
  16.3 0.1 copy-done
  16.4 1.0 convert_reduce_fusion.1
  17.3 18.8 %all_gather.10 = f32[8,4,128]{2,1,0:T(4,128)S(1)} all-gather(f32[1,4,128]{2,1,0:T(4,128)S(1)} %bitcast.34), channel_id=1, replica_groups=mesh['seq'=8,'head'=4] {'seq'}, dimensions={0}, use_global_device_ids=true | all-gather | bytes 18432 | tf_op jit(solution)/shard_map/all_gather | solution.py:28
  36.1 0.1 multiply_reduce_fusion.1
  36.3 0.0 copy-done.5
  36.3 2.5 %fusion.16 = f32[4,4,1,256]{3,2,1,0:T(1,128)S(1)} fusion(f32[4,4,128,1]{2,3,1,0:T(1,128)S(1)} %bitcast.35, bf16[4,256,4,128]{3,2,1,0:T(4,128)(2,1)S(1)} %reshape.45), kind=kOutput, calls=%fused_computation.31 | convolution fusion | flops 8912896 | bytes 1073152 | tf_op jit(solution)/shard_map/sthd,shd->sth/dot_general | solution.py:43
  38.8 0.0 copy-done.1
  38.8 0.7 fusion.31
  39.6 0.0 copy-start.4
  39.6 1.2 %fusion.47 = (f32[4,4,256]{2,1,0:T(4,128)S(1)}, f32[4,4,256,256]{2,3,1,0:T(8,128)S(1)}) fusion(f32[4,4,256,256]{2,3,1,0:T(8,128)S(1)} %fusion.31, pred[256,256]{0,1:T(8,128)(4,1)S(1)} %iota_compare_fusion), kind=kOutput, calls=%fused_computation.65 | output fusion | flops 6291711 | bytes 8470528 | tf_op jit(solution)/shard_map/sub | solution.py:50
  40.8 0.0 copy-done.4
  40.8 1.9 %fusion.14 = f32[4,4,256,128]{2,3,1,0:T(8,128)} fusion(f32[4,4,256,256]{2,3,1,0:T(8,128)S(1)} %get-tuple-element.8, f32[4,4,256]{2,1,0:T(4,128)S(1)} %get-tuple-element.7, bf16[4,256,4,128]{3,2,1,0:T(4,128)(2,1)S(1)} %copy-done.4), kind=kOutput, calls=%fused_computation.28 | convolution fusion | flops 270532608 | bytes 7356416 | tf_op jit(solution)/shard_map/shqk,skhd->sqhd/dot_general | solution.py:51
  42.7 0.0 slice-start
  42.7 19.1 %all-gather.6.cloned.1.call-done = f32[32,128,128]{2,1,0:T(8,128)} async-done(((f32[4,128,128]{2,1,0:T(8,128)}), f32[32,128,128]{2,1,0:T(8,128)}) %all-gather.6.cloned.1.call-update) | async-done | bytes 2097168 | tf_op jit(solution)/shard_map/all_gather | solution.py:27
  61.8 1.9 %multiply_reduce_fusion = f32[4,128,128]{2,1,0:T(8,128)S(1)} fusion(f32[8,4,128,128]{3,2,1,0:T(8,128)} %bitcast.33, f32[8]{0:T(128)S(1)} %compare_convert_fusion), kind=kLoop, calls=%fused_computation.27 | loop fusion | flops 983040 | bytes 2359328 | tf_op jit(solution)/shard_map/reduce_sum | solution.py:32
  63.6 0.0 slice-done
  63.7 4.7 %fusion.10 = bf16[4,256,4,128]{1,3,2,0:T(8,128)(2,1)S(1)} fusion(f32[4,4,256,128]{2,3,1,0:T(8,128)} %fusion.14, f32[4]{0:T(128)S(1)} %get-tuple-element.5, f32[4,256,4]{1,2,0:T(4,128)S(1)} %fusion.38, f32[3,4,128,128]{3,2,1,0:T(8,128)S(1)} %slice-done, f32[4]{0:T(128)S(1)} %get-tuple-element.6, bf16[4,256,4,128]{3,2,1,0:T(4,128)(2,1)S(1)} %reshape.45, ...), kind=kOutput, calls=%fused_computation.20 | convolution fusion | flops 810811392 | bytes 5259296 | tf_op jit(solution)/shard_map/sthd,shde->sthe/dot_general | solution.py:42
  68.4 0.7 copy.37
  69.0 1.2 copy.71
  70.2 0.0 all-gather.4.cloned.1.call-update
  70.2 35.6 %all-gather.4.cloned.1.call-done = bf16[1024,2048]{1,0:T(8,128)(2,1)} async-done(((bf16[1024,512]{1,0:T(8,128)(2,1)}), bf16[1024,2048]{1,0:T(8,128)(2,1)}) %all-gather.4.cloned.1.call-update) | async-done | bytes 4194320 | tf_op jit(solution)/shard_map/all_gather | solution.py:60
  105.8 9.3 %convolution_convert_fusion = bf16[1024,1024]{1,0:T(8,128)(2,1)} fusion(bf16[1024,2048]{1,0:T(8,128)(2,1)} %all-gather.4.cloned.1.call-done, bf16[2048,1024]{1,0:T(8,128)(2,1)} %param.9), kind=kOutput, calls=%fused_computation.30 | convolution fusion | flops 4296015872 | bytes 10485760 | tf_op jit(solution)/shard_map/dot_general | solution.py:59
  (7 shorter events, 0.1 us)
Async XLA Ops:
  6.5 1.5 %copy-start.2 = (bf16[1024,512]{1,0:T(8,128)(2,1)S(1)}, bf16[1024,512]{1,0:T(8,128)(2,1)}, u32[]{:S(2)}) copy-start(bf16[1024,512]{1,0:T(8,128)(2,1)} %param.7) | copy-start | bytes 3145732
  6.5 55.2 %all-gather.6.cloned.1.call-start = ((), (), s32[]{:S(2)}) async-start(), calls=%async_computation.1 | async-start | bytes 2359296 | tf_op jit(solution)/shard_map/all_gather | solution.py:27
  9.2 4.4 %copy-start.3 = (bf16[1024,512]{1,0:T(8,128)(2,1)S(1)}, bf16[1024,512]{1,0:T(8,128)(2,1)}, u32[]{:S(2)}) copy-start(bf16[1024,512]{1,0:T(8,128)(2,1)} %param.5) | copy-start | bytes 3145732
  13.5 92.3 %all-gather.4.cloned.1.call-start = ((), (), s32[]{:S(2)}) async-start(), calls=%async_computation | async-start | bytes 5242880 | tf_op jit(solution)/shard_map/all_gather | solution.py:60
  14.8 1.5 %copy-start = (bf16[1024,512]{1,0:T(8,128)(2,1)S(1)}, bf16[1024,512]{1,0:T(8,128)(2,1)}, u32[]{:S(2)}) copy-start(bf16[1024,512]{1,0:T(8,128)(2,1)} %param.6) | copy-start | bytes 3145732
  14.9 21.4 %copy-start.5 = (f32[4]{0:T(128)S(1)}, f32[4]{0:T(128)}, u32[]{:S(2)}) copy-start(f32[4]{0:T(128)} %param.8) | copy-start | bytes 52
  16.3 22.6 %copy-start.1 = (f32[4,4,128,128]{3,2,1,0:T(8,128)}, f32[4,4,128,128]{3,2,1,0:T(8,128)S(1)}, u32[]{:S(2)}) copy-start(f32[4,4,128,128]{3,2,1,0:T(8,128)S(1)} %fusion.49) | copy-start | bytes 3145732
  39.6 1.3 %copy-start.4 = (bf16[4,256,4,128]{3,2,1,0:T(4,128)(2,1)S(1)}, bf16[4,256,4,128]{3,2,1,0:T(4,128)(2,1)}, u32[]{:S(2)}) copy-start(bf16[4,256,4,128]{3,2,1,0:T(4,128)(2,1)} %reshape.44) | copy-start | bytes 3145732
  42.7 20.9 %slice-start = ((f32[4,4,128,128]{3,2,1,0:T(8,128)}), f32[3,4,128,128]{3,2,1,0:T(8,128)S(1)}, s32[]{:S(2)}) async-start(f32[4,4,128,128]{3,2,1,0:T(8,128)} %copy-done.1), calls=%async_computation.2 | async-start | bytes 1572864 | tf_op jit(solution)/shard_map/slice | solution.py:35
Sparse Core Ops, SparseCore 0:
  13.6 48.1 all-gather.5
  70.3 35.3 all-gather.3
where the time goes:
time: 124 us; the launch traced here: 122 us
  waiting for transfers between devices  54.6 us (44%)
  matrix products  23.4 us (19%)
  blocking collectives  18.8 us (15%)
  between operations  13.6 us (11%)
  other arithmetic  6.57 us (5%)
  local copies, waits for them, and re-layouts  4.86 us (4%)
    all_gather x1, waiting for transfers between devices, body(): lax.all_gather(context, 'head', axis=1, tiled=True)  35.6 us
    all_gather x1, waiting for transfers between devices, body(): lax.all_gather(mem_total[None], 'seq', axis=0, tiled=True)  19.1 us
    all_gather x1, blocking collectives, body(): lax.all_gather(norm_total[None], 'seq', axis=0, tiled=True)  18.8 us
    dot_general x1, matrix products, body(): jnp.dot(lax.all_gather(context, 'head', axis=1, tiled=True), out_weight,...  9.27 us
    dot_general x1, matrix products, body(): recall = jnp.einsum('sthd,shde->sthe', query_map, mem_prev, precision=high)  4.69 us
    dot_general x1, matrix products, body(): jnp.einsum('sthd,sthe->shde', key_map, value_blk, preferred_element_type=...  4.29 us
    dot_general x1, matrix products, body(): jnp.einsum('sthd,shd->sth', query_map, norm_prev, precision=high) + 1.0  2.52 us
  transfers between devices with their start and end apart: 2, of which 2 were waited for; matrix products, arithmetic and copies ran while one was open for 8% of the time, Pallas kernels for 0%

commit v1 on v0

v1 whole, which is shorter than its diff:
```python
import functools

import jax
import jax.numpy as jnp
from jax import lax
from jax.experimental import pallas as pl
from jax.experimental.pallas import tpu as pltpu
from jax.sharding import PartitionSpec as P

DH = 128
SEG = 256
MEM = DH + 8
PAIR = 2 * DH
MESH = pl.DeviceIdType.MESH
F32 = jnp.float32
BF16 = jnp.bfloat16
NT = (((1,), (1,)), ((), ()))
TN = (((0,), (0,)), ((), ()))


def elu1(x):
    return jnp.where(x > 0.0, x + 1.0, jnp.exp(jnp.minimum(x, 0.0)))


def split(x):
    top = x.astype(BF16)
    return top, (x - top.astype(F32)).astype(BF16)


def kernel(
    ns, nh, q_ref, k_ref, v_ref, gate_ref, w_hbm, out_ref,
    w_ref, local, inner, total, from_pair, from_prev, to_next, prior, ctx, acc,
    w_sem, x_send, x_recv, z_send, z_recv, c_send, c_recv, f_send,
):
    rows, cols = q_ref.shape
    segs, heads = rows // SEG, cols // DH
    pairs = heads // 2
    blocks = segs * heads
    me_s, me_h = lax.axis_index("seq"), lax.axis_index("head")
    z, odd = me_s // 2, lax.rem(me_s, 2)
    zs = ns // 2
    pair_s = me_s + 1 - 2 * odd
    up, down = lax.rem(me_s + 2, ns), lax.rem(me_s + ns - 2, ns)
    group, core = me_h // 2, lax.rem(me_h, 2)
    pair_h = me_h + 1 - 2 * core
    groups = nh // 2

    weight_copy = pltpu.make_async_copy(w_hbm, w_ref, w_sem)
    weight_copy.start()

    barrier = pltpu.get_barrier_semaphore()
    seq_peers = [pair_s, up, down]
    for s in seq_peers:
        pl.semaphore_signal(barrier, inc=1, device_id=(s, me_h), device_id_type=MESH)
    far = [lax.rem(group + d, groups) * 2 + core for d in range(1, groups)]
    for h in [pair_h] + far:
        pl.semaphore_signal(barrier, inc=1, device_id=(me_s, h), device_id_type=MESH)

    def x_copy(h):
        return pltpu.make_async_remote_copy(
            src_ref=total.at[h], dst_ref=from_pair.at[h],
            send_sem=x_send.at[h], recv_sem=x_recv.at[h],
            device_id=(pair_s, me_h), device_id_type=MESH,
        )

    def z_copy(h):
        return pltpu.make_async_remote_copy(
            src_ref=to_next.at[h], dst_ref=from_prev.at[h],
            send_sem=z_send.at[h], recv_sem=z_recv.at[h],
            device_id=(up, me_h), device_id_type=MESH,
        )

    def ctx_copy(source, target, j, s, send):
        part = ctx.at[source * pairs + j, pl.ds(pl.multiple_of(s * SEG, SEG), SEG)]
        return pltpu.make_async_remote_copy(
            src_ref=part, dst_ref=part,
            send_sem=send, recv_sem=c_recv.at[source, j, s],
            device_id=(me_s, target), device_id_type=MESH,
        )

    for h in range(heads):
        span = pl.ds(h * DH, DH)
        run = jnp.zeros((MEM, DH), F32)
        for s in range(segs):
            inner[h, s] = run
            part = pl.ds(s * SEG, SEG)
            key_map = elu1(k_ref[part, span].astype(F32)).astype(BF16)
            delta = lax.dot_general(v_ref[part, span], key_map, TN, preferred_element_type=F32)
            norm = jnp.sum(key_map.astype(F32), axis=0, keepdims=True)
            run = run + jnp.concatenate([delta, jnp.broadcast_to(norm, (8, DH))], axis=0)
        total[h] = run
        if h == 0:
            pl.semaphore_wait(barrier, 3 + 1 + len(far))
        x_copy(h).start()

    @pl.when(z == 0)
    def _():
        from_prev[...] = jnp.zeros_like(from_prev)

    def chain(h):
        x_copy(h).wait_recv()

        @pl.when(z > 0)
        def _():
            z_copy(h).wait_recv()

        before = from_prev[h]
        other = from_pair[h]

        @pl.when(z < zs - 1)
        def _():
            to_next[h] = before + (total[h] + other)
            z_copy(h).start()

        prior[h] = before + jnp.where(odd == 1, other, 0.0)

    row_id = lax.broadcasted_iota(jnp.int32, (SEG, SEG), 0)
    col_id = lax.broadcasted_iota(jnp.int32, (SEG, SEG), 1)
    ones = jnp.ones((SEG, DH), BF16)
    first, hop = 3, 5

    @pl.loop(0, blocks)
    def _(b):
        for c in range(heads):
            @pl.when(b == first + 2 * c + hop * z)
            def _():
                chain(c)
        h, s = b // segs, lax.rem(b, segs)
        span = pl.ds(pl.multiple_of(h * DH, DH), DH)
        part = pl.ds(pl.multiple_of(s * SEG, SEG), SEG)
        scores = lax.dot_general(q_ref[part, span], k_ref[part, span], NT, preferred_element_type=F32)
        scores = jnp.where(row_id >= col_id, scores * (1.0 / DH**0.5), -1e30)
        weights = jnp.exp(scores - jnp.max(scores, axis=1, keepdims=True)).astype(BF16)
        both = jnp.dot(
            weights, jnp.concatenate([v_ref[part, span], ones], axis=1), preferred_element_type=F32
        )
        local[part, span] = both[:, :DH] / both[:, DH:]

    for c in range(heads):
        @pl.when(first + 2 * c + hop * z >= blocks)
        def _():
            chain(c)

    for j in range(pairs):
        gates = [
            1.0 / (1.0 + jnp.exp(-jnp.full((1, DH), gate_ref[2 * j + i], F32))) for i in range(2)
        ]

        @pl.loop(0, segs)
        def _(s):
            part = pl.ds(pl.multiple_of(s * SEG, SEG), SEG)
            mixed = []
            for i in range(2):
                h = 2 * j + i
                span = pl.ds(h * DH, DH)
                mem = prior[h] + inner[h, s]
                mem = jnp.concatenate(
                    [mem[:DH], jnp.broadcast_to(mem[DH : DH + 1], (DH, DH))], axis=0
                )
                m_top, m_low = split(mem)
                q_top, q_low = split(elu1(q_ref[part, span].astype(F32)))
                recall = lax.dot_general(
                    jnp.concatenate([q_top, q_low], axis=1),
                    jnp.concatenate([m_top, m_top], axis=1),
                    NT, preferred_element_type=F32,
                ) + lax.dot_general(q_top, m_low, NT, preferred_element_type=F32)
                recall = recall[:, :DH] / (recall[:, DH:] + 1.0)
                mixed.append(gates[i] * recall + (1.0 - gates[i]) * local[part, span])
            ctx[me_h * pairs + j, part] = jnp.concatenate(mixed, axis=1).astype(BF16)
            for t in far + [pair_h]:
                ctx_copy(me_h, t, j, s, c_send.at[t, j, s]).start()

    weight_copy.wait()

    def product(source, j, part):
        slot = source * pairs + j
        return jnp.dot(
            ctx[slot, part],
            w_ref[pl.ds(pl.multiple_of(slot * PAIR, PAIR), PAIR), :],
            preferred_element_type=F32,
        )

    @pl.loop(0, segs)
    def _(s):
        part = pl.ds(pl.multiple_of(s * SEG, SEG), SEG)
        for j in range(pairs):
            ctx_copy(pair_h, pair_h, j, s, c_send.at[pair_h, j, s]).wait_recv()
        sums = product(me_h, 0, part)
        for j in range(1, pairs):
            sums = sums + product(me_h, j, part)
        for j in range(pairs):
            sums = sums + product(pair_h, j, part)
        acc[part, :] = sums

    for j in range(pairs):
        for f in far:
            twin = (f // 2) * 2 + 1 - core

            @pl.loop(0, segs)
            def _(s):
                part = pl.ds(pl.multiple_of(s * SEG, SEG), SEG)
                ctx_copy(f, pair_h, j, s, c_send.at[f, j, s]).wait_recv()
                ctx_copy(f, pair_h, j, s, f_send.at[f, j, s]).start()
                sums = acc[part, :] + product(f, j, part)
                ctx_copy(twin, pair_h, j, s, c_send.at[f, j, s]).wait_recv()
                acc[part, :] = sums + product(twin, j, part)

    out_ref[...] = acc[...].astype(BF16)

    for h in range(heads):
        x_copy(h).wait_send()

        @pl.when(z < zs - 1)
        def _():
            z_copy(h).wait_send()

    for j in range(pairs):
        @pl.loop(0, segs)
        def _(s):
            for t in far + [pair_h]:
                ctx_copy(me_h, t, j, s, c_send.at[t, j, s]).wait_send()
            for f in far:
                ctx_copy(f, pair_h, j, s, f_send.at[f, j, s]).wait_send()


def body(ns, nh, queries, keys, values, gate_bias, out_weight):
    rows, cols = queries.shape
    depth, outs = out_weight.shape
    segs, heads = rows // SEG, cols // DH
    pairs = heads // 2
    vmem = pl.BlockSpec(memory_space=pltpu.VMEM)
    dma = pltpu.SemaphoreType.DMA
    mem = pltpu.VMEM((heads, MEM, DH), F32)
    return pl.pallas_call(
        functools.partial(kernel, ns, nh),
        out_shape=jax.ShapeDtypeStruct((rows, outs), BF16),
        in_specs=[vmem, vmem, vmem, pl.BlockSpec(memory_space=pltpu.SMEM),
                  pl.BlockSpec(memory_space=pl.ANY)],
        out_specs=vmem,
        scratch_shapes=[
            pltpu.VMEM((depth, outs), BF16),
            pltpu.VMEM((rows, cols), F32),
            pltpu.VMEM((heads, segs, MEM, DH), F32),
            mem, mem, mem, mem, mem,
            pltpu.VMEM((nh * pairs, rows, PAIR), BF16),
            pltpu.VMEM((rows, outs), F32),
            dma, dma((heads,)), dma((heads,)), dma((heads,)), dma((heads,)),
            dma((nh, pairs, segs)), dma((nh, pairs, segs)), dma((nh, pairs, segs)),
        ],
        compiler_params=pltpu.CompilerParams(
            collective_id=0, has_side_effects=True, vmem_limit_bytes=60 * 1024 * 1024
        ),
        name="infini_layer",
    )(queries, keys, values, gate_bias, out_weight)


def solution(mesh):
    sizes = dict(mesh.shape)
    return jax.shard_map(
        functools.partial(body, sizes["seq"], sizes["head"]),
        mesh=mesh,
        in_specs=(P("seq", "head"), P("seq", "head"), P("seq", "head"), P("head"), P(None, "head")),
        out_specs=P("seq", "head"),
        check_vma=False,
    )
```

time: 124 us -> 52.7 us (0.43); the launches traced: 122 us -> 52.5 us
  waiting for transfers between devices: 54.6 us -> 0 us
  Pallas kernels: 0 us -> 49.4 us
  matrix products: 23.4 us -> 0 us
  blocking collectives: 18.8 us -> 0 us
  between operations: 13.6 us -> 0.01 us
  other arithmetic: 6.57 us -> 0 us
  local copies, waits for them, and re-layouts: 4.86 us -> 3.08 us
    all_gather x2 -> x0, waiting for transfers between devices: 54.6 us -> none  [the longest x1 35.6 us: body(): lax.all_gather(context, 'head', axis=1, tiled=True)]
    pallas_call x0 -> x1, Pallas kernels: none -> 49.4 us  [body(): pl.pallas_call(functools.partial(kernel, ns, nh), out_shape=jax.ShapeDtyp...]
    dot_general x6 -> x0, matrix products: 23.4 us -> none  [the longest x1 9.27 us: body(): jnp.dot(lax.all_gather(context, 'head', axis=1, tiled=True), out_weight,...]
    all_gather x1 -> x0, blocking collectives: 18.8 us -> none  [body(): lax.all_gather(norm_total[None], 'seq', axis=0, tiled=True)]
    reduce_sum x4 -> x0, other arithmetic: 3.88 us -> none  [the longest x1 1.85 us: body(): mem_part = jnp.sum(pieces[0] * keep_mask[:, None, None, None], axis=0)]
    reshape x3 -> x0, local copies, waits for them, and re-layouts: 2.81 us -> none  [the longest x1 1.43 us: body(): key_blk = keys.reshape(blk_shape)]
    unnamed x13 -> x1, local copies, waits for them, and re-layouts: 1.37 us -> 3.08 us
    another operation x2 -> x0, other arithmetic: 1.39 us -> none  [the longest x1 1.38 us: body(): jnp.cumsum(deltas, axis=0)[:-1]]
  transfers between devices with their start and end apart: 2 -> 0, of which waited for: 2 -> 0; matrix products, arithmetic and copies ran while one was open for 8% -> 0% of each run, Pallas kernels for 0% -> 0%
where the time goes in v1:
time: 52.7 us; the launch traced here: 52.5 us
  Pallas kernels  49.4 us (94%)
  local copies, waits for them, and re-layouts  3.08 us (6%)
    pallas_call x1, Pallas kernels, body(): pl.pallas_call(functools.partial(kernel, ns, nh), out_shape=jax.ShapeDtyp...  49.4 us
    unnamed x1, local copies, waits for them, and re-layouts  3.08 us

profile of v1, /device:TPU:25, one launch (start us, length us, event | category | flops | bytes accessed | tf_op | source)
XLA Modules:
  0.0 52.5 jit_solution(7627174808739633525)
XLA Ops:
  0.0 49.4 %infini_layer.1 = bf16[1024,1024]{1,0:T(8,128)(2,1)} custom-call(bf16[1024,512]{1,0:T(8,128)(2,1)} %q_ref.1, bf16[1024,512]{1,0:T(8,128)(2,1)} %k_ref.1, bf16[1024,512]{1,0:T(8,128)(2,1)} %v_ref.1, f32[4]{0:T(128)} %gate_ref.1, bf16[2048,1024]{1,0:T(8,128)(2,1)} %w_hbm.1), custom_call_target="tpu_custom_call" | custom-call | tf_op jit(solution)/shard_map/infini_layer/pallas_call | solution.py:234
  49.4 3.1 %copy.7 = bf16[1024,1024]{1,0:T(8,128)(2,1)} copy(bf16[1024,1024]{1,0:T(8,128)(2,1)} %infini_layer.1) | data formatting | bytes 4194304
